TPU v7x, 32 devices: a whole 2x2x4 slice. The times are simulated.
32 devices in a mesh: groups: 2 (over y), dp: 4 (over z), section: 2 (over x), tensor: 2 (over core).
Axes of the slice: x: 2, y: 2, z: 4, core: 2. Of those that a mesh axis runs over, the one named last changes fastest.
Arguments:
- hidden: bfloat16 [128, 8, 5120], P(('groups', 'dp')), parts along dimension 0, may hold values from -6 to 6
- unembed: bfloat16 [128, 8, 5120], P(('groups', 'dp')), parts along dimension 0, may hold values from -0.02734375 to 0.02734375
- value_proj: bfloat16 [2, 5120, 512], P('section', 'dp', 'tensor'), may hold values from -0.078125 to 0.078125
- output_proj: bfloat16 [2, 512, 5120], P('section', 'tensor', 'dp'), may hold values from -0.125 to 0.125
- norm_gains: float32 [2, 5120], P('section'), may hold values from 0.1 to 1.9
- survive: int32 [8], P(('groups', 'dp')), parts along dimension 0, may hold values from 0 to 1, as said below
- lengths: int32 [128], P(('groups', 'dp')), parts along dimension 0, may hold values from 1 to 8
- assign: int32 [128], P(('groups', 'dp')), parts along dimension 0, may hold values from 0 to 16, as said below
- advantage: float32 [128], P(('groups', 'dp')), parts along dimension 0, may hold values from -4 to 4
- reference_logit: float32 [128, 8], P(('groups', 'dp')), parts along dimension 0, may hold values from -4 to 4
- recorded_gap: float32 [128, 8], P(('groups', 'dp')), parts along dimension 0, may hold values from -2 to 2
Outputs:
- grad_value: float32 [4, 5120, 512], P(('groups', 'section'), 'dp', 'tensor'), parts along dimension 0
- grad_output: float32 [4, 512, 5120], P(('groups', 'section'), 'tensor', 'dp'), parts along dimension 0
There are 2 independent parts, one for each index of `groups`. A program takes and returns all parts, laid end to end along the dimension named above; an argument that names none is the same for every part. Nothing has to cross between parts.
Inputs may be any that keep to these rules, and one draw needn't show every extreme that they name: `survive`: 1 where the group of 16 responses is kept, 0 where it is dropped; in every draw all groups of some dp index are kept. `assign`: the 16 slots of a dp index list the local positions (0 to 15) of the responses of its kept groups, each exactly once, then hold 16 in every other slot.
All inputs are finite; a program needn't handle non-finite values.
Results may differ from a plain program's by a relative error of at most 0.029.
Values may be sent and summed in bfloat16 or wider, within the bound.
A program may use at most 64 MiB of HBM per device.

v0:
```python
import math
import jax
import jax.numpy as jnp
from jax import lax
from jax.sharding import PartitionSpec as P

GROUP = 16
MB_RESP = 8
eps_norm = 1e-06
loss_scale = 4096.0
clip_high = math.log(1.28)
clip_low = math.log(0.8)


def from_behind(block, axis, distance):
    devices = range(lax.axis_size(axis))
    route = [(i - distance, i) for i in devices if i - distance in devices]
    return lax.ppermute(block, axis, route)


def norm_forward(row_block, norm_gain):
    values = row_block.astype(jnp.float32)
    inverse = lax.rsqrt(jnp.mean(values * values, axis=-1, keepdims=True) + eps_norm)
    return (values, inverse, (values * inverse * norm_gain).astype(jnp.bfloat16))


def norm_backward(values, inverse, norm_gain, upstream):
    scaled = upstream * norm_gain
    inner_sum = jnp.sum(scaled * values, axis=-1, keepdims=True) / values.shape[-1]
    return inverse * scaled - values * (inverse * inverse * inverse) * inner_sum


def contract_last(left_rows, right_rows):
    return lax.dot_general(
        left_rows, right_rows, (((1,), (1,)), ((), ())), preferred_element_type=jnp.float32
    )


def contract_first(left_rows, right_rows):
    return lax.dot_general(
        left_rows, right_rows, (((0,), (0,)), ((), ())), preferred_element_type=jnp.float32
    )


def take_slot(slot_store, slot_index):
    return lax.dynamic_index_in_dim(slot_store, slot_index, 0, keepdims=False)


def put_slot(slot_store, new_value, slot_index, active):
    previous = take_slot(slot_store, slot_index)
    return lax.dynamic_update_index_in_dim(
        slot_store, jnp.where(active, new_value, previous), slot_index, 0
    )


def local(
    hidden,
    unembed,
    value_proj,
    output_proj,
    norm_gains,
    survive,
    lengths,
    assign,
    advantage,
    reference_logit,
    recorded_gap,
):
    resp_count = hidden.shape[0]
    positions = hidden.shape[1]
    model_width = hidden.shape[2]
    half_value = value_proj.shape[2]
    micro_count = resp_count // MB_RESP
    row_count = MB_RESP * positions
    section_count = lax.axis_size("section")
    section_index = lax.axis_index("section")
    is_last = section_index == section_count - 1
    norm_gain = norm_gains[0]
    alive_mask = jnp.repeat(survive, GROUP)
    local_count = jnp.sum((alive_mask * lengths).astype(jnp.float32))
    gathered_value, gathered_output = (
        lax.all_gather(value_proj, "dp", axis=1, tiled=True),
        lax.all_gather(output_proj, "dp", axis=2, tiled=True),
    )
    w_first = gathered_value[0]
    w_second = gathered_output[0]

    def pick(array):
        return jnp.take(array, assign, axis=0, mode="fill", fill_value=0)

    slot_hidden = pick(hidden).reshape(micro_count, row_count, model_width)
    slot_unembed = pick(unembed).reshape(micro_count, row_count, model_width)
    position_index = lax.broadcasted_iota(jnp.int32, (resp_count, positions), 1)
    live_mask = (position_index < pick(lengths)[:, None]).astype(jnp.float32)
    advantages = jnp.broadcast_to(pick(advantage)[:, None], (resp_count, positions))
    gap_rows = pick(recorded_gap)
    clipped = (advantages > 0) & (gap_rows > clip_high) | (advantages < 0) & (gap_rows < clip_low)
    kept_mask = 1.0 - clipped.astype(jnp.float32)
    weight_rows = (-loss_scale * advantages * kept_mask * live_mask).reshape(micro_count, row_count)
    logit_base = pick(reference_logit).reshape(micro_count, row_count)
    step_count = micro_count + section_count - 1
    store_in = jnp.zeros((micro_count, row_count, model_width), jnp.bfloat16)
    store_normed = jnp.zeros((micro_count, row_count, model_width), jnp.bfloat16)
    store_projected = jnp.zeros((micro_count, row_count, half_value), jnp.bfloat16)
    store_out = jnp.zeros((micro_count, row_count, model_width), jnp.bfloat16)
    arriving = jnp.zeros((row_count, model_width), jnp.bfloat16)
    for step_index in range(step_count):
        micro_index = step_index - section_index
        active = (micro_index >= 0) & (micro_index < micro_count)
        clamped = jnp.clip(micro_index, 0, micro_count - 1)
        entering = jnp.where(section_index == 0, take_slot(slot_hidden, clamped), arriving)
        values, inverse, normed = norm_forward(entering, norm_gain)
        projected = jnp.dot(normed, w_first, preferred_element_type=jnp.float32).astype(
            jnp.bfloat16
        )
        partial_out = jnp.dot(projected, w_second, preferred_element_type=jnp.float32)
        mixed_sum = lax.psum(partial_out.astype(jnp.bfloat16), "tensor").astype(jnp.float32)
        leaving = (values + mixed_sum).astype(jnp.bfloat16)
        store_in = put_slot(store_in, entering, clamped, active)
        store_normed = put_slot(store_normed, normed, clamped, active)
        store_projected = put_slot(store_projected, projected, clamped, active)
        store_out = put_slot(store_out, leaving, clamped, active)
        arriving = from_behind(leaving, "section", 1)
    store_upstream = jnp.zeros((micro_count, row_count, model_width), jnp.bfloat16)
    store_grad_value = jnp.zeros((micro_count, row_count, half_value), jnp.bfloat16)
    arriving = jnp.zeros((row_count, model_width), jnp.bfloat16)
    for step_index in range(step_count):
        micro_index = step_index - (section_count - 1 - section_index)
        active = (micro_index >= 0) & (micro_index < micro_count)
        clamped = jnp.clip(micro_index, 0, micro_count - 1)
        top_rows = take_slot(store_out, clamped).astype(jnp.float32)
        unembed_rows = take_slot(slot_unembed, clamped).astype(jnp.float32)
        logit = jnp.sum(top_rows * unembed_rows, axis=-1)
        seed_rows = take_slot(weight_rows, clamped) * jnp.exp(
            logit - take_slot(logit_base, clamped)
        )
        start_grad = (seed_rows[:, None] * unembed_rows).astype(jnp.bfloat16)
        upstream = jnp.where(is_last, start_grad, arriving)
        entering = take_slot(store_in, clamped)
        normed = take_slot(store_normed, clamped)
        projected = take_slot(store_projected, clamped)
        grad_projected = contract_last(upstream, w_second).astype(jnp.bfloat16)
        partial_norm = contract_last(grad_projected, w_first)
        grad_normed = lax.psum(partial_norm.astype(jnp.bfloat16), "tensor").astype(jnp.float32)
        values, inverse, unused_normed = norm_forward(entering, norm_gain)
        grad_entering = (
            upstream.astype(jnp.float32) + norm_backward(values, inverse, norm_gain, grad_normed)
        ).astype(jnp.bfloat16)
        store_upstream = put_slot(store_upstream, upstream, clamped, active)
        store_grad_value = put_slot(store_grad_value, grad_projected, clamped, active)
        arriving = from_behind(grad_entering, "section", -1)
    flat_normed = store_normed.reshape(micro_count * row_count, model_width)
    flat_upstream = store_upstream.reshape(micro_count * row_count, model_width)
    flat_grad_value = store_grad_value.reshape(micro_count * row_count, half_value)
    flat_projected = store_projected.reshape(micro_count * row_count, half_value)
    reduced = lax.psum_scatter(
        jnp.concatenate(
            [
                contract_first(flat_normed, flat_grad_value),
                contract_first(flat_upstream, flat_projected),
            ],
            axis=1,
        ).astype(jnp.bfloat16),
        "dp",
        scatter_dimension=0,
        tiled=True,
    ).astype(jnp.float32)
    token_total = lax.psum(local_count, "dp")
    scaled_grads = reduced / token_total
    grad_value = scaled_grads[:, :half_value][None]
    grad_output = scaled_grads[:, half_value:].T[None]
    return (grad_value, grad_output)


def solution(mesh):
    placed = (
        P(("groups", "dp"), None, None),
        P(("groups", "dp"), None, None),
        P("section", "dp", "tensor"),
        P("section", "tensor", "dp"),
        P("section", None),
        P(("groups", "dp")),
        P(("groups", "dp")),
        P(("groups", "dp")),
        P(("groups", "dp")),
        P(("groups", "dp"), None),
        P(("groups", "dp"), None),
    )
    return jax.shard_map(
        local,
        mesh=mesh,
        in_specs=placed,
        out_specs=(
            P(("groups", "section"), "dp", "tensor"),
            P(("groups", "section"), "tensor", "dp"),
        ),
        check_vma=False,
    )
```

profile of v0, /device:TPU:0, one launch (start us, length us, event | category | flops | bytes accessed | tf_op | source)
XLA Modules:
  0.0 449.3 jit_solution(629598408572374933)
XLA Ops:
  9.5 1.7 gather_fusion.2
  11.2 1.7 gather_fusion.4
  14.8 2.0 broadcast_select_fusion.1
  16.8 1.0 copy-done.12
  18.2 48.9 %all-gather.3.cloned.1.call-done = bf16[1,5120,256]{2,1,0:T(8,128)(2,1)} async-done(((bf16[1,1280,256]{2,1,0:T(8,128)(2,1)}), bf16[1,5120,256]{2,1,0:T(8,128)(2,1)}) %all-gather.3.cloned.1.call-update) | async-done | bytes 2621456 | tf_op jit(solution)/shard_map/all_gather | solution.py:82
  67.1 2.6 bitcast_dynamic-update-slice_fusion.10
  69.7 52.5 %all-gather.5.cloned.1.call-done = bf16[1,256,5120]{2,1,0:T(8,128)(2,1)} async-done(((bf16[1,256,1280]{2,1,0:T(8,128)(2,1)}), bf16[1,256,5120]{2,1,0:T(8,128)(2,1)}) %all-gather.5.cloned.1.call-update) | async-done | bytes 2621456 | tf_op jit(solution)/shard_map/all_gather | solution.py:83
  122.2 3.2 convolution_convert_fusion.4
  125.7 1.2 broadcast.209.clone
  127.5 1.0 select_dynamic-update-slice_fusion.1
  128.5 14.6 %all-reduce.6.cloned.1.call-done = bf16[64,5120]{1,0:T(8,128)(2,1)} async-done(((bf16[64,5120]{1,0:T(8,128)(2,1)}), bf16[64,5120]{1,0:T(8,128)(2,1)}) %all-reduce.6.cloned.1.call-update) | async-done | bytes 655376 | tf_op jit(solution)/shard_map/psum | solution.py:117
  143.2 1.2 copy-done.14
  144.4 1.4 bitcast_dynamic-update-slice_fusion.5
  145.8 3.7 collective-permute-start
  149.5 1.1 constant_dynamic-slice_fusion.9
  150.7 13.2 %collective-permute-done = bf16[64,5120]{1,0:T(8,128)(2,1)S(1)} collective-permute-done((bf16[64,5120]{1,0:T(8,128)(2,1)S(1)}, bf16[64,5120]{1,0:T(8,128)(2,1)S(1)}, u32[]{:S(2)}, u32[]{:S(2)}) %collective-permute-start) | collective-permute-done | bytes 655392 | tf_op jit(solution)/shard_map/ppermute | solution.py:18
  163.9 1.1 bitcast_dynamic-update-slice_fusion.3
  165.9 1.1 copy-done.3
  167.0 1.5 convolution_convert_fusion.3
  168.6 2.0 constant_dynamic-slice_fusion.14
  170.6 2.0 constant_dynamic-slice_fusion.8
  172.6 16.8 %all-reduce.8.cloned.1.call-done = bf16[64,5120]{1,0:T(8,128)(2,1)} async-done(((bf16[64,5120]{1,0:T(8,128)(2,1)}), bf16[64,5120]{1,0:T(8,128)(2,1)}) %all-reduce.8.cloned.1.call-update) | async-done | bytes 655376 | tf_op jit(solution)/shard_map/psum | solution.py:117
  189.4 2.5 bitcast_dynamic-update-slice_fusion.4
  191.9 3.7 collective-permute-start.1
  195.6 2.2 constant_dynamic-slice_fusion.13
  197.8 12.1 %collective-permute-done.1 = bf16[64,5120]{1,0:T(8,128)(2,1)S(1)} collective-permute-done((bf16[64,5120]{1,0:T(8,128)(2,1)S(1)}, bf16[64,5120]{1,0:T(8,128)(2,1)S(1)}, u32[]{:S(2)}, u32[]{:S(2)}) %collective-permute-start.1) | collective-permute-done | bytes 655392 | tf_op jit(solution)/shard_map/ppermute | solution.py:18
  210.1 1.4 bitcast_dynamic-update-slice_fusion.2
  212.8 1.1 copy-done.4
  213.9 1.4 convolution_convert_fusion.2
  215.4 1.2 constant_dynamic-slice_fusion.17
  217.3 1.1 copy-done.18
  218.4 0.9 constant_dynamic-slice_fusion.16
  219.3 17.0 %all-reduce.10.cloned.1.call-done = bf16[64,5120]{1,0:T(8,128)(2,1)} async-done(((bf16[64,5120]{1,0:T(8,128)(2,1)}), bf16[64,5120]{1,0:T(8,128)(2,1)}) %all-reduce.10.cloned.1.call-update) | async-done | bytes 655376 | tf_op jit(solution)/shard_map/psum | solution.py:117
  236.2 3.1 bitcast_dynamic-update-slice_fusion.6
  239.3 2.4 fusion.32
  241.8 0.9 bitcast_dynamic-update-slice_fusion.12
  243.5 1.7 convolution_convert_fusion.1
  245.3 1.2 broadcast.209
  246.5 1.1 select_dynamic-update-slice_fusion
  247.6 17.8 %all-reduce.12.cloned.1.call-done = bf16[64,5120]{1,0:T(8,128)(2,1)} async-done(((bf16[64,5120]{1,0:T(8,128)(2,1)}), bf16[64,5120]{1,0:T(8,128)(2,1)}) %all-reduce.12.cloned.1.call-update) | async-done | bytes 655376 | tf_op jit(solution)/shard_map/psum | solution.py:144
  265.4 2.1 fusion.48
  267.6 1.6 fusion.46
  269.2 1.5 collective-permute-start.2
  270.7 1.1 constant_dynamic-slice_fusion.3
  271.8 16.1 %collective-permute-done.2 = bf16[64,5120]{1,0:T(8,128)(2,1)S(1)} collective-permute-done((bf16[64,5120]{1,0:T(8,128)(2,1)S(1)}, bf16[64,5120]{1,0:T(8,128)(2,1)S(1)}, u32[]{:S(2)}, u32[]{:S(2)}) %collective-permute-start.2) | collective-permute-done | bytes 655392 | tf_op jit(solution)/shard_map/ppermute | solution.py:18
  288.0 1.2 bitcast_dynamic-update-slice_fusion.1
  290.0 0.9 bitcast_dynamic-update-slice_fusion.11
  291.7 1.7 convolution_convert_fusion
  293.5 19.2 %all-reduce.14.cloned.1.call-done = bf16[64,5120]{1,0:T(8,128)(2,1)} async-done(((bf16[64,5120]{1,0:T(8,128)(2,1)}), bf16[64,5120]{1,0:T(8,128)(2,1)}) %all-reduce.14.cloned.1.call-update) | async-done | bytes 655376 | tf_op jit(solution)/shard_map/psum | solution.py:144
  312.7 1.7 fusion.53
  314.4 1.7 fusion.52
  316.1 1.3 collective-permute-start.3
  317.4 1.1 constant_dynamic-slice_fusion.2
  318.6 16.3 %collective-permute-done.3 = bf16[64,5120]{1,0:T(8,128)(2,1)S(1)} collective-permute-done((bf16[64,5120]{1,0:T(8,128)(2,1)S(1)}, bf16[64,5120]{1,0:T(8,128)(2,1)S(1)}, u32[]{:S(2)}, u32[]{:S(2)}) %collective-permute-start.3) | collective-permute-done | bytes 655392 | tf_op jit(solution)/shard_map/ppermute | solution.py:18
  334.9 0.9 fusion.78
  336.2 0.9 fusion
  337.1 1.2 bitcast_dynamic-update-slice_fusion
  338.3 2.2 fusion.1
  340.5 2.7 pad_maximum_fusion
  344.5 12.9 %psum.47 = f32[]{:T(128)} all-reduce(f32[]{:T(128)} %convert_reduce_fusion), channel_id=1, replica_groups=mesh['groups'=2,'dp'=4,'section'=2,'tensor'=2] {'dp'}, use_global_device_ids=true, to_apply=%region_17.20 | all-reduce | flops 1 | bytes 8 | tf_op jit(solution)/shard_map/psum | solution.py:168
  357.4 80.2 %reduce-scatter.2.cloned.1.call-done = bf16[1280,512]{0,1:T(8,128)(2,1)} async-done(((bf16[5120,512]{0,1:T(8,128)(2,1)}), bf16[1280,512]{0,1:T(8,128)(2,1)}) %reduce-scatter.2.cloned.1.call-update) | async-done | bytes 1310736 | tf_op jit(solution)/shard_map/reduce_scatter | solution.py:156
  437.6 2.2 convert_divide_fusion
  439.7 1.2 slice_bitcast_fusion
  441.0 1.5 copy.18
  (110 shorter events, 12.1 us)
Async XLA Ops:
  7.2 2.3 copy-start
  7.2 1.6 copy-start.30
  7.2 1.6 copy-start.1
  7.2 59.9 %all-gather.3.cloned.1.call-start = ((), (), s32[]{:S(2)}) async-start(), calls=%async_computation.1 | async-start | bytes 3276800 | tf_op jit(solution)/shard_map/all_gather | solution.py:82
  7.9 114.3 %all-gather.5.cloned.1.call-start = ((), (), s32[]{:S(2)}) async-start(), calls=%async_computation.2 | async-start | bytes 3276800 | tf_op jit(solution)/shard_map/all_gather | solution.py:83
  8.7 134.4 %all-reduce.6.cloned.1.call-start = ((), (), s32[]{:S(2)}) async-start(), calls=%async_computation.3 | async-start | bytes 1310720 | tf_op jit(solution)/shard_map/psum | solution.py:117
  9.5 1.7 copy-start.27
  11.2 1.7 copy-start.2
  11.2 2.4 copy-start.28
  11.2 3.0 copy-start.29
  14.8 52.3 %copy-start.26 = (f32[1,5120]{1,0:T(1,128)S(1)}, f32[1,5120]{1,0:T(1,128)}, u32[]{:S(2)}) copy-start(f32[1,5120]{1,0:T(1,128)} %param.19) | copy-start | bytes 61444
  16.8 1.1 copy-start.12
  125.4 64.0 %all-reduce.8.cloned.1.call-start = ((), (), s32[]{:S(2)}) async-start(), calls=%async_computation.4 | async-start | bytes 1310720 | tf_op jit(solution)/shard_map/psum | solution.py:117
  125.7 1.8 copy-start.13
  143.1 1.3 copy-start.14
  145.8 4.9 %copy-start.20 = (bf16[2,64,5120]{2,1,0:T(8,128)(2,1)}, bf16[2,64,5120]{2,1,0:T(8,128)(2,1)S(1)}, u32[]{:S(2)}) copy-start(bf16[2,64,5120]{2,1,0:T(8,128)(2,1)S(1)} %get-tuple-element.22) | copy-start | bytes 3932164
  145.8 18.1 %collective-permute-start = (bf16[64,5120]{1,0:T(8,128)(2,1)S(1)}, bf16[64,5120]{1,0:T(8,128)(2,1)S(1)}, u32[]{:S(2)}, u32[]{:S(2)}) collective-permute-start(bf16[64,5120]{1,0:T(8,128)(2,1)S(1)} %get-tuple-element.23), channel_id=1, source_target_pairs={{0,2},{1,3},{4,6},{5,7},{8,10},{9,11},{12,14},{13,15},{16,18},{17,... | collective-permute-start | bytes 1966088 | tf_op jit(solution)/shard_map/ppermute | solution.py:18
  150.7 14.6 %copy-start.8 = (bf16[1,5120,256]{2,1,0:T(8,128)(2,1)S(1)}, bf16[1,5120,256]{2,1,0:T(8,128)(2,1)}, u32[]{:S(2)}) copy-start(bf16[1,5120,256]{2,1,0:T(8,128)(2,1)} %all-gather.3.cloned.1.call-done) | copy-start | bytes 7864324
  165.3 1.7 copy-start.3
  168.5 67.7 %all-reduce.10.cloned.1.call-start = ((), (), s32[]{:S(2)}) async-start(), calls=%async_computation.5 | async-start | bytes 1310720 | tf_op jit(solution)/shard_map/psum | solution.py:117
  191.9 18.1 %collective-permute-start.1 = (bf16[64,5120]{1,0:T(8,128)(2,1)S(1)}, bf16[64,5120]{1,0:T(8,128)(2,1)S(1)}, u32[]{:S(2)}, u32[]{:S(2)}) collective-permute-start(bf16[64,5120]{1,0:T(8,128)(2,1)S(1)} %get-tuple-element.21), channel_id=1, source_target_pairs={{0,2},{1,3},{4,6},{5,7},{8,10},{9,11},{12,14},{13,15},{16,18},{17,... | collective-permute-start | bytes 1966088 | tf_op jit(solution)/shard_map/ppermute | solution.py:18
  195.6 14.5 %copy-start.15 = (bf16[16,8,5120]{2,1,0:T(8,128)(2,1)S(1)}, bf16[16,8,5120]{2,1,0:T(8,128)(2,1)}, u32[]{:S(2)}) copy-start(bf16[16,8,5120]{2,1,0:T(8,128)(2,1)} %copy-done.12) | copy-start | bytes 3932164
  195.6 14.5 %copy-start.25 = (bf16[1,64,5120]{2,1,0:T(8,128)(2,1)S(1)}, bf16[1,64,5120]{2,1,0:T(8,128)(2,1)}, u32[]{:S(2)}) copy-start(bf16[1,64,5120]{2,1,0:T(8,128)(2,1)} %constant_dynamic-slice_fusion.8) | copy-start | bytes 1966084
  210.1 2.0 copy-start.9
  211.5 1.2 copy-start.16
  211.5 1.3 copy-start.21
  212.0 1.9 copy-start.4
  215.4 50.0 %all-reduce.12.cloned.1.call-start = ((), (), s32[]{:S(2)}) async-start(), calls=%async_computation.6 | async-start | bytes 1310720 | tf_op jit(solution)/shard_map/psum | solution.py:144
  215.4 1.5 copy-start.17
  217.3 1.1 copy-start.18
  218.4 17.8 %copy-start.22 = (bf16[64,5120]{1,0:T(8,128)(2,1)S(1)}, bf16[64,5120]{1,0:T(8,128)(2,1)}, u32[]{:S(2)}) copy-start(bf16[64,5120]{1,0:T(8,128)(2,1)} %copy-done.21) | copy-start | bytes 1966084
  239.3 2.4 copy-start.5
  241.8 1.7 copy-start.10
  245.3 67.4 %all-reduce.14.cloned.1.call-start = ((), (), s32[]{:S(2)}) async-start(), calls=%async_computation.7 | async-start | bytes 1310720 | tf_op jit(solution)/shard_map/psum | solution.py:144
  265.4 2.1 copy-start.24
  269.2 18.8 %collective-permute-start.2 = (bf16[64,5120]{1,0:T(8,128)(2,1)S(1)}, bf16[64,5120]{1,0:T(8,128)(2,1)S(1)}, u32[]{:S(2)}, u32[]{:S(2)}) collective-permute-start(bf16[64,5120]{1,0:T(8,128)(2,1)S(1)} %fusion.46), channel_id=1, source_target_pairs={{2,0},{3,1},{6,4},{7,5},{10,8},{11,9},{14,12},{15,13},{18,16},{19,... | collective-permute-start | bytes 1966088 | tf_op jit(solution)/shard_map/ppermute | solution.py:18
  288.0 2.0 copy-start.6
  290.0 1.7 copy-start.11
  293.5 144.1 %reduce-scatter.2.cloned.1.call-start = ((), (), s32[]{:S(2)}) async-start(), calls=%async_computation.8 | async-start | bytes 6553600 | tf_op jit(solution)/shard_map/reduce_scatter | solution.py:156
  312.7 1.7 copy-start.23
  314.4 20.5 %copy-start.7 = (bf16[1,256,5120]{2,1,0:T(8,128)(2,1)S(1)}, bf16[1,256,5120]{2,1,0:T(8,128)(2,1)}, u32[]{:S(2)}) copy-start(bf16[1,256,5120]{2,1,0:T(8,128)(2,1)} %all-gather.5.cloned.1.call-done) | copy-start | bytes 7864324
  316.1 18.8 %collective-permute-start.3 = (bf16[64,5120]{1,0:T(8,128)(2,1)S(1)}, bf16[64,5120]{1,0:T(8,128)(2,1)S(1)}, u32[]{:S(2)}, u32[]{:S(2)}) collective-permute-start(bf16[64,5120]{1,0:T(8,128)(2,1)S(1)} %fusion.52), channel_id=1, source_target_pairs={{2,0},{3,1},{6,4},{7,5},{10,8},{11,9},{14,12},{15,13},{18,16},{19,... | collective-permute-start | bytes 1966088 | tf_op jit(solution)/shard_map/ppermute | solution.py:18
  334.9 1.3 copy-start.19
Sparse Core Ops, SparseCore 0:
  9.6 57.4 all-gather.2
  68.6 53.4 all-gather.4
  125.5 17.5 all-reduce.5
  168.6 20.6 all-reduce.7
  215.5 20.6 all-reduce.9
  245.4 19.9 all-reduce.11
  293.6 19.0 all-reduce.13
  343.3 94.1 reduce-scatter.1
where the time goes:
time: 450 us; the launch traced here: 449 us
  waiting for transfers between devices  326 us (72%)
  local copies, waits for them, and re-layouts  32.9 us (7%)
  other arithmetic  32.2 us (7%)
  matrix products  19.3 us (4%)
  between operations  15.3 us (3%)
  blocking collectives  12.9 us (3%)
  starting transfers between devices  10.5 us (2%)
    reduce_scatter x1, waiting for transfers between devices, local(): lax.psum_scatter(jnp.concatenate([contract_first(flat_normed, flat_grad_v...  80.2 us
    ppermute x4, waiting for transfers between devices, from_behind(): return lax.ppermute(block, axis, route)  57.8 us
    all_gather x1, waiting for transfers between devices, local(): lax.all_gather(output_proj, 'dp', axis=2, tiled=True)  52.5 us
    all_gather x1, waiting for transfers between devices, local(): lax.all_gather(value_proj, 'dp', axis=1, tiled=True)  48.9 us
    psum x3, waiting for transfers between devices, local(): lax.psum(partial_out.astype(jnp.bfloat16), 'tensor').astype(jnp.float32)  48.4 us
    psum x2, waiting for transfers between devices, local(): lax.psum(partial_norm.astype(jnp.bfloat16), 'tensor').astype(jnp.float32)  37 us
    dynamic_update_slice x10, other arithmetic, put_slot(): lax.dynamic_update_index_in_dim(slot_store, jnp.where(active, new_value,...  14.3 us
    psum x1, blocking collectives, local(): token_total = lax.psum(local_count, 'dp')  12.9 us
  transfers between devices with their start and end apart: 12, of which 12 were waited for; matrix products, arithmetic and copies ran while one was open for 6% of the time, Pallas kernels for 0%

commit v1 on v0

--- a/solution.py
+++ b/solution.py
@@ -80,7 +80,7 @@
     local_count = jnp.sum((alive_mask * lengths).astype(jnp.float32))
     gathered_value, gathered_output = (
         lax.all_gather(value_proj, "dp", axis=1, tiled=True),
-        lax.all_gather(output_proj, "dp", axis=2, tiled=True),
+        jnp.concatenate(lax.all_gather(output_proj, "dp"), axis=2),
     )
     w_first = gathered_value[0]
     w_second = gathered_output[0]

time: 450 us -> 453 us (level)
  local copies, waits for them, and re-layouts: 32.9 us -> 38.6 us
    unnamed x65 -> x67, local copies, waits for them, and re-layouts: 11.3 us -> 12.6 us
  transfers between devices with their start and end apart: 12 -> 12, of which waited for: 12 -> 12; matrix products, arithmetic and copies ran while one was open for 6% -> 7% of each run, Pallas kernels for 0% -> 0%
where the time goes in v1:
time: 453 us; the launch traced here: 452 us
  waiting for transfers between devices  324 us (72%)
  local copies, waits for them, and re-layouts  38.6 us (9%)
  other arithmetic  32.2 us (7%)
  matrix products  17.7 us (4%)
  between operations  15.4 us (3%)
  blocking collectives  12.9 us (3%)
  starting transfers between devices  10.5 us (2%)
    reduce_scatter x1, waiting for transfers between devices, local(): lax.psum_scatter(jnp.concatenate([contract_first(flat_normed, flat_grad_v...  80.1 us
    ppermute x4, waiting for transfers between devices, from_behind(): return lax.ppermute(block, axis, route)  57.8 us
    all_gather x1, waiting for transfers between devices, local(): lax.all_gather(value_proj, 'dp', axis=1, tiled=True)  50.8 us
    all_gather x1, waiting for transfers between devices, local(): lax.all_gather(output_proj, 'dp')  48.9 us
    psum x3, waiting for transfers between devices, local(): lax.psum(partial_out.astype(jnp.bfloat16), 'tensor').astype(jnp.float32)  48.4 us
    psum x2, waiting for transfers between devices, local(): lax.psum(partial_norm.astype(jnp.bfloat16), 'tensor').astype(jnp.float32)  37 us
    dynamic_update_slice x10, other arithmetic, put_slot(): lax.dynamic_update_index_in_dim(slot_store, jnp.where(active, new_value,...  14.3 us
    psum x1, blocking collectives, local(): token_total = lax.psum(local_count, 'dp')  12.9 us
  transfers between devices with their start and end apart: 12, of which 12 were waited for; matrix products, arithmetic and copies ran while one was open for 7% of the time, Pallas kernels for 0%

profile of v1, /device:TPU:0, one launch (start us, length us, event | category | flops | bytes accessed | tf_op | source)
XLA Modules:
  0.0 451.7 jit_solution(9021176902481455351)
XLA Ops:
  9.5 1.7 gather_fusion.2
  11.2 1.7 gather_fusion.4
  14.8 2.0 broadcast_select_fusion.1
  16.8 1.0 copy-done.13
  18.2 48.9 %all-gather.6.cloned.1.call-done = bf16[4,256,1280]{2,1,0:T(8,128)(2,1)} async-done(((bf16[1,256,1280]{2,1,0:T(8,128)(2,1)}), bf16[4,256,1280]{2,1,0:T(8,128)(2,1)}) %all-gather.6.cloned.1.call-update) | async-done | bytes 2621456 | tf_op jit(solution)/shard_map/all_gather | solution.py:83
  67.1 4.4 copy.20
  71.5 50.8 %all-gather.4.cloned.1.call-done = bf16[1,5120,256]{2,1,0:T(8,128)(2,1)} async-done(((bf16[1,1280,256]{2,1,0:T(8,128)(2,1)}), bf16[1,5120,256]{2,1,0:T(8,128)(2,1)}) %all-gather.4.cloned.1.call-update) | async-done | bytes 2621456 | tf_op jit(solution)/shard_map/all_gather | solution.py:82
  122.2 2.7 bitcast_dynamic-update-slice_fusion.10
  125.0 1.8 convolution_convert_fusion.4
  127.1 1.2 broadcast.209.clone
  128.9 1.0 select_dynamic-update-slice_fusion.1
  129.9 14.6 %all-reduce.6.cloned.1.call-done = bf16[64,5120]{1,0:T(8,128)(2,1)} async-done(((bf16[64,5120]{1,0:T(8,128)(2,1)}), bf16[64,5120]{1,0:T(8,128)(2,1)}) %all-reduce.6.cloned.1.call-update) | async-done | bytes 655376 | tf_op jit(solution)/shard_map/psum | solution.py:117
  144.6 1.2 copy-done.15
  145.8 1.4 bitcast_dynamic-update-slice_fusion.5
  147.2 3.7 collective-permute-start
  150.9 1.1 constant_dynamic-slice_fusion.9
  152.1 13.2 %collective-permute-done = bf16[64,5120]{1,0:T(8,128)(2,1)S(1)} collective-permute-done((bf16[64,5120]{1,0:T(8,128)(2,1)S(1)}, bf16[64,5120]{1,0:T(8,128)(2,1)S(1)}, u32[]{:S(2)}, u32[]{:S(2)}) %collective-permute-start) | collective-permute-done | bytes 655392 | tf_op jit(solution)/shard_map/ppermute | solution.py:18
  165.3 1.1 bitcast_dynamic-update-slice_fusion.3
  167.3 1.1 copy-done.4
  168.4 1.8 convolution_convert_fusion.3
  170.3 2.0 constant_dynamic-slice_fusion.14
  172.3 2.0 constant_dynamic-slice_fusion.8
  174.3 16.8 %all-reduce.8.cloned.1.call-done = bf16[64,5120]{1,0:T(8,128)(2,1)} async-done(((bf16[64,5120]{1,0:T(8,128)(2,1)}), bf16[64,5120]{1,0:T(8,128)(2,1)}) %all-reduce.8.cloned.1.call-update) | async-done | bytes 655376 | tf_op jit(solution)/shard_map/psum | solution.py:117
  191.1 2.5 bitcast_dynamic-update-slice_fusion.4
  193.6 3.7 collective-permute-start.1
  197.3 2.2 constant_dynamic-slice_fusion.13
  199.5 12.1 %collective-permute-done.1 = bf16[64,5120]{1,0:T(8,128)(2,1)S(1)} collective-permute-done((bf16[64,5120]{1,0:T(8,128)(2,1)S(1)}, bf16[64,5120]{1,0:T(8,128)(2,1)S(1)}, u32[]{:S(2)}, u32[]{:S(2)}) %collective-permute-start.1) | collective-permute-done | bytes 655392 | tf_op jit(solution)/shard_map/ppermute | solution.py:18
  211.8 1.4 bitcast_dynamic-update-slice_fusion.2
  214.9 1.1 copy-done.5
  216.0 1.8 convolution_convert_fusion.2
  217.9 1.2 constant_dynamic-slice_fusion.17
  219.7 1.1 copy-done.19
  220.8 0.9 constant_dynamic-slice_fusion.16
  221.7 17.0 %all-reduce.10.cloned.1.call-done = bf16[64,5120]{1,0:T(8,128)(2,1)} async-done(((bf16[64,5120]{1,0:T(8,128)(2,1)}), bf16[64,5120]{1,0:T(8,128)(2,1)}) %all-reduce.10.cloned.1.call-update) | async-done | bytes 655376 | tf_op jit(solution)/shard_map/psum | solution.py:117
  238.7 3.1 bitcast_dynamic-update-slice_fusion.6
  241.7 2.4 fusion.23
  244.8 1.1 copy-done.11
  245.9 1.8 convolution_convert_fusion.1
  247.8 1.2 broadcast.209
  248.9 1.1 select_dynamic-update-slice_fusion
  250.0 17.8 %all-reduce.12.cloned.1.call-done = bf16[64,5120]{1,0:T(8,128)(2,1)} async-done(((bf16[64,5120]{1,0:T(8,128)(2,1)}), bf16[64,5120]{1,0:T(8,128)(2,1)}) %all-reduce.12.cloned.1.call-update) | async-done | bytes 655376 | tf_op jit(solution)/shard_map/psum | solution.py:144
  267.9 2.1 fusion.39
  270.0 1.6 fusion.37
  271.6 1.5 collective-permute-start.2
  273.1 1.1 constant_dynamic-slice_fusion.3
  274.3 16.1 %collective-permute-done.2 = bf16[64,5120]{1,0:T(8,128)(2,1)S(1)} collective-permute-done((bf16[64,5120]{1,0:T(8,128)(2,1)S(1)}, bf16[64,5120]{1,0:T(8,128)(2,1)S(1)}, u32[]{:S(2)}, u32[]{:S(2)}) %collective-permute-start.2) | collective-permute-done | bytes 655392 | tf_op jit(solution)/shard_map/ppermute | solution.py:18
  290.4 1.2 bitcast_dynamic-update-slice_fusion.1
  293.0 1.2 copy-done.12
  294.1 1.7 convolution_convert_fusion
  296.0 19.2 %all-reduce.14.cloned.1.call-done = bf16[64,5120]{1,0:T(8,128)(2,1)} async-done(((bf16[64,5120]{1,0:T(8,128)(2,1)}), bf16[64,5120]{1,0:T(8,128)(2,1)}) %all-reduce.14.cloned.1.call-update) | async-done | bytes 655376 | tf_op jit(solution)/shard_map/psum | solution.py:144
  315.2 1.7 fusion.44
  316.9 1.7 fusion.43
  318.6 1.3 collective-permute-start.3
  319.9 1.1 constant_dynamic-slice_fusion.2
  321.0 16.3 %collective-permute-done.3 = bf16[64,5120]{1,0:T(8,128)(2,1)S(1)} collective-permute-done((bf16[64,5120]{1,0:T(8,128)(2,1)S(1)}, bf16[64,5120]{1,0:T(8,128)(2,1)S(1)}, u32[]{:S(2)}, u32[]{:S(2)}) %collective-permute-start.3) | collective-permute-done | bytes 655392 | tf_op jit(solution)/shard_map/ppermute | solution.py:18
  338.7 0.9 fusion
  339.6 1.2 bitcast_dynamic-update-slice_fusion
  340.7 2.2 fusion.1
  343.0 2.7 pad_maximum_fusion
  346.9 12.9 %psum.47 = f32[]{:T(128)} all-reduce(f32[]{:T(128)} %convert_reduce_fusion), channel_id=1, replica_groups=mesh['groups'=2,'dp'=4,'section'=2,'tensor'=2] {'dp'}, use_global_device_ids=true, to_apply=%region_17.20 | all-reduce | flops 1 | bytes 8 | tf_op jit(solution)/shard_map/psum | solution.py:168
  359.9 80.1 %reduce-scatter.2.cloned.1.call-done = bf16[1280,512]{0,1:T(8,128)(2,1)} async-done(((bf16[5120,512]{0,1:T(8,128)(2,1)}), bf16[1280,512]{0,1:T(8,128)(2,1)}) %reduce-scatter.2.cloned.1.call-update) | async-done | bytes 1310736 | tf_op jit(solution)/shard_map/reduce_scatter | solution.py:156
  440.0 2.2 convert_divide_fusion
  442.2 1.2 slice_bitcast_fusion
  443.4 1.5 copy.23
  (113 shorter events, 13.0 us)
Async XLA Ops:
  7.2 2.3 copy-start
  7.2 1.6 copy-start.31
  7.2 1.6 copy-start.1
  7.2 59.9 %all-gather.6.cloned.1.call-start = ((), (), s32[]{:S(2)}) async-start(), calls=%async_computation.8 | async-start | bytes 3276800 | tf_op jit(solution)/shard_map/all_gather | solution.py:83
  7.9 114.3 %all-gather.4.cloned.1.call-start = ((), (), s32[]{:S(2)}) async-start(), calls=%async_computation.1 | async-start | bytes 3276800 | tf_op jit(solution)/shard_map/all_gather | solution.py:82
  8.7 135.8 %all-reduce.6.cloned.1.call-start = ((), (), s32[]{:S(2)}) async-start(), calls=%async_computation.2 | async-start | bytes 1310720 | tf_op jit(solution)/shard_map/psum | solution.py:117
  9.5 1.7 copy-start.28
  11.2 1.7 copy-start.2
  11.2 2.4 copy-start.29
  11.2 3.0 copy-start.30
  16.8 1.1 copy-start.13
  18.2 104.1 %copy-start.27 = (f32[1,5120]{1,0:T(1,128)S(1)}, f32[1,5120]{1,0:T(1,128)}, u32[]{:S(2)}) copy-start(f32[1,5120]{1,0:T(1,128)} %param.19) | copy-start | bytes 61444
  122.2 2.7 copy-start.3
  126.8 64.3 %all-reduce.8.cloned.1.call-start = ((), (), s32[]{:S(2)}) async-start(), calls=%async_computation.3 | async-start | bytes 1310720 | tf_op jit(solution)/shard_map/psum | solution.py:117
  127.1 1.8 copy-start.14
  144.5 1.3 copy-start.15
  147.2 4.9 %copy-start.21 = (bf16[2,64,5120]{2,1,0:T(8,128)(2,1)}, bf16[2,64,5120]{2,1,0:T(8,128)(2,1)S(1)}, u32[]{:S(2)}) copy-start(bf16[2,64,5120]{2,1,0:T(8,128)(2,1)S(1)} %get-tuple-element.24) | copy-start | bytes 3932164
  147.2 18.1 %collective-permute-start = (bf16[64,5120]{1,0:T(8,128)(2,1)S(1)}, bf16[64,5120]{1,0:T(8,128)(2,1)S(1)}, u32[]{:S(2)}, u32[]{:S(2)}) collective-permute-start(bf16[64,5120]{1,0:T(8,128)(2,1)S(1)} %get-tuple-element.25), channel_id=1, source_target_pairs={{0,2},{1,3},{4,6},{5,7},{8,10},{9,11},{12,14},{13,15},{16,18},{17,... | collective-permute-start | bytes 1966088 | tf_op jit(solution)/shard_map/ppermute | solution.py:18
  152.1 14.6 %copy-start.9 = (bf16[1,5120,256]{2,1,0:T(8,128)(2,1)S(1)}, bf16[1,5120,256]{2,1,0:T(8,128)(2,1)}, u32[]{:S(2)}) copy-start(bf16[1,5120,256]{2,1,0:T(8,128)(2,1)} %all-gather.4.cloned.1.call-done) | copy-start | bytes 7864324
  166.7 1.7 copy-start.4
  170.2 68.4 %all-reduce.10.cloned.1.call-start = ((), (), s32[]{:S(2)}) async-start(), calls=%async_computation.4 | async-start | bytes 1310720 | tf_op jit(solution)/shard_map/psum | solution.py:117
  193.6 18.0 %collective-permute-start.1 = (bf16[64,5120]{1,0:T(8,128)(2,1)S(1)}, bf16[64,5120]{1,0:T(8,128)(2,1)S(1)}, u32[]{:S(2)}, u32[]{:S(2)}) collective-permute-start(bf16[64,5120]{1,0:T(8,128)(2,1)S(1)} %get-tuple-element.23), channel_id=1, source_target_pairs={{0,2},{1,3},{4,6},{5,7},{8,10},{9,11},{12,14},{13,15},{16,18},{17,... | collective-permute-start | bytes 1966088 | tf_op jit(solution)/shard_map/ppermute | solution.py:18
  197.3 14.5 %copy-start.16 = (bf16[16,8,5120]{2,1,0:T(8,128)(2,1)S(1)}, bf16[16,8,5120]{2,1,0:T(8,128)(2,1)}, u32[]{:S(2)}) copy-start(bf16[16,8,5120]{2,1,0:T(8,128)(2,1)} %copy-done.13) | copy-start | bytes 3932164
  197.3 14.5 %copy-start.26 = (bf16[1,64,5120]{2,1,0:T(8,128)(2,1)S(1)}, bf16[1,64,5120]{2,1,0:T(8,128)(2,1)}, u32[]{:S(2)}) copy-start(bf16[1,64,5120]{2,1,0:T(8,128)(2,1)} %constant_dynamic-slice_fusion.8) | copy-start | bytes 1966084
  211.8 2.5 copy-start.10
  213.2 1.1 copy-start.17
  213.2 1.7 copy-start.22
  214.3 1.7 copy-start.5
  217.8 50.0 %all-reduce.12.cloned.1.call-start = ((), (), s32[]{:S(2)}) async-start(), calls=%async_computation.5 | async-start | bytes 1310720 | tf_op jit(solution)/shard_map/psum | solution.py:144
  217.9 1.5 copy-start.18
  219.7 1.1 copy-start.19
  220.8 17.9 %copy-start.23 = (bf16[64,5120]{1,0:T(8,128)(2,1)S(1)}, bf16[64,5120]{1,0:T(8,128)(2,1)}, u32[]{:S(2)}) copy-start(bf16[64,5120]{1,0:T(8,128)(2,1)} %copy-done.22) | copy-start | bytes 1966084
  241.7 2.4 copy-start.6
  244.2 1.7 copy-start.11
  247.7 67.4 %all-reduce.14.cloned.1.call-start = ((), (), s32[]{:S(2)}) async-start(), calls=%async_computation.6 | async-start | bytes 1310720 | tf_op jit(solution)/shard_map/psum | solution.py:144
  267.9 2.1 copy-start.25
  271.6 18.8 %collective-permute-start.2 = (bf16[64,5120]{1,0:T(8,128)(2,1)S(1)}, bf16[64,5120]{1,0:T(8,128)(2,1)S(1)}, u32[]{:S(2)}, u32[]{:S(2)}) collective-permute-start(bf16[64,5120]{1,0:T(8,128)(2,1)S(1)} %fusion.37), channel_id=1, source_target_pairs={{2,0},{3,1},{6,4},{7,5},{10,8},{11,9},{14,12},{15,13},{18,16},{19,... | collective-permute-start | bytes 1966088 | tf_op jit(solution)/shard_map/ppermute | solution.py:18
  290.4 2.0 copy-start.7
  292.4 1.7 copy-start.12
  295.9 144.1 %reduce-scatter.2.cloned.1.call-start = ((), (), s32[]{:S(2)}) async-start(), calls=%async_computation.7 | async-start | bytes 6553600 | tf_op jit(solution)/shard_map/reduce_scatter | solution.py:156
  315.2 1.7 copy-start.24
  316.8 20.5 %copy-start.8 = (bf16[4,256,1280]{1,2,0:T(8,128)(2,1)S(1)}, bf16[4,256,1280]{1,2,0:T(8,128)(2,1)}, u32[]{:S(2)}) copy-start(bf16[4,256,1280]{1,2,0:T(8,128)(2,1)} %copy.20) | copy-start | bytes 7864324
  318.6 18.8 %collective-permute-start.3 = (bf16[64,5120]{1,0:T(8,128)(2,1)S(1)}, bf16[64,5120]{1,0:T(8,128)(2,1)S(1)}, u32[]{:S(2)}, u32[]{:S(2)}) collective-permute-start(bf16[64,5120]{1,0:T(8,128)(2,1)S(1)} %fusion.43), channel_id=1, source_target_pairs={{2,0},{3,1},{6,4},{7,5},{10,8},{11,9},{14,12},{15,13},{18,16},{19,... | collective-permute-start | bytes 1966088 | tf_op jit(solution)/shard_map/ppermute | solution.py:18
  337.4 1.3 copy-start.20
Sparse Core Ops, SparseCore 0:
  9.6 57.4 all-gather.5
  68.6 53.5 all-gather.3
  126.9 17.5 all-reduce.5
  170.4 20.6 all-reduce.7
  217.9 20.6 all-reduce.9
  247.8 19.9 all-reduce.11
  296.0 19.0 all-reduce.13
  345.8 94.1 reduce-scatter.1
